TPU v7x, 1024 devices: a whole 8x8x8 slice. The times are simulated.
1024 devices in a mesh: blk: 512 (over z, y, x), uly: 2 (over core).
Axes of the slice: x: 8, y: 8, z: 8, core: 2. Of those that a mesh axis runs over, the one named last changes fastest.
Arguments:
- queries: bfloat16 [98304, 8192], P(('blk', 'uly')), may hold values from -300 to 300
- keys: bfloat16 [98304, 1024], P(('blk', 'uly')), may hold values from -4 to 4
- values: bfloat16 [98304, 1024], P(('blk', 'uly')), may hold values from -6 to 6
- doc_lengths: int32 [1024], replicated, may hold values from 1 to 384, as said below
Outputs:
- attention: bfloat16 [98304, 8192], P(('blk', 'uly'))
Inputs may be any that keep to these rules, and one draw needn't show every extreme that they name: `doc_lengths`: every document has 1 to 384 tokens, the lengths sum to 98304, and some document has exactly 384 tokens.
All inputs are finite; a program needn't handle non-finite values.
Results may differ from a plain program's by a relative error of at most 0.003.
Values may be sent and summed in bfloat16 or wider, within the bound.
A program may use at most 32 MiB of HBM per device.

v0:
```python
import jax
import jax.numpy as jnp
from jax import lax
from jax.sharding import PartitionSpec as P

HEADS = 64
KV_HEADS = 8
HEAD_DIM = 128
REACH = 2


MASKED = -1e30


def from_behind(value, axis, by):
    size = lax.axis_size(axis)
    pairs = [(i, i + by) for i in range(size) if 0 <= i + by < size]
    return lax.ppermute(value, axis, pairs)


def doc_index(positions, starts):
    return jnp.sum((positions[:, None] >= starts[None, :]).astype(jnp.int32), axis=1) - 1


def fold_block(running, grouped, query_pos, query_doc, key_block, value_block, anchor, starts):
    block_rows = key_block.shape[0]
    running_max, row_total, weighted = running
    key_pos = anchor * block_rows + jnp.arange(block_rows, dtype=jnp.int32)
    key_doc = doc_index(key_pos, starts)
    allowed = (key_doc[None, :] == query_doc[:, None]) & (key_pos[None, :] <= query_pos[:, None])
    heads_kv = key_block.shape[1] // HEAD_DIM
    key_heads = key_block.reshape(block_rows, heads_kv, HEAD_DIM).transpose(1, 0, 2)
    value_heads = value_block.reshape(block_rows, heads_kv, HEAD_DIM).transpose(1, 0, 2)
    scores = jnp.einsum(
        "gqd,gkd->gqk", grouped, key_heads, preferred_element_type=jnp.float32
    ) * HEAD_DIM ** (-0.5)
    scores = jnp.where(allowed[None], scores, jnp.float32(MASKED))
    new_max = jnp.maximum(running_max, jnp.max(scores, axis=-1))
    rescale = jnp.exp(running_max - new_max)
    weights = jnp.exp(scores - new_max[..., None])
    row_total = row_total * rescale + jnp.sum(weights, axis=-1)
    rounded = weights.astype(jnp.bfloat16)
    weighted = weighted * rescale[..., None] + jnp.einsum(
        "gqk,gkd->gqd", rounded, value_heads, preferred_element_type=jnp.float32
    )
    return (new_max, row_total, weighted)


def local(queries, keys, values, doc_lengths):
    local_queries, local_keys, local_values = (
        lax.all_to_all(queries, "uly", split_axis=1, concat_axis=0, tiled=True),
        lax.all_to_all(keys, "uly", split_axis=1, concat_axis=0, tiled=True),
        lax.all_to_all(values, "uly", split_axis=1, concat_axis=0, tiled=True),
    )
    block_rows = local_queries.shape[0]
    heads_kv = local_keys.shape[1] // HEAD_DIM
    group_size = HEADS // KV_HEADS
    query_rows = block_rows * group_size
    shard_index = lax.axis_index("blk")
    starts = jnp.cumsum(doc_lengths) - doc_lengths
    grouped = local_queries.reshape(block_rows, heads_kv, group_size, HEAD_DIM).transpose(
        1, 0, 2, 3
    )
    grouped = grouped.reshape(heads_kv, query_rows, HEAD_DIM)
    query_pos = shard_index * block_rows + jnp.arange(query_rows, dtype=jnp.int32) // group_size
    query_doc = doc_index(query_pos, starts)
    stacked = jnp.stack([local_keys, local_values])
    fetched = [from_behind(stacked, "blk", distance) for distance in range(1, REACH + 1)]
    running = (
        jnp.full((heads_kv, query_rows), MASKED, jnp.float32),
        jnp.zeros((heads_kv, query_rows), jnp.float32),
        jnp.zeros((heads_kv, query_rows, HEAD_DIM), jnp.float32),
    )
    running = fold_block(
        running, grouped, query_pos, query_doc, local_keys, local_values, shard_index, starts
    )
    for distance in range(1, REACH + 1):
        anchor = shard_index - distance
        incoming = fetched[distance - 1]
        running = fold_block(
            running, grouped, query_pos, query_doc, incoming[0], incoming[1], anchor, starts
        )
    result = (running[2] / running[1][..., None]).astype(jnp.bfloat16)
    result = result.reshape(heads_kv, block_rows, group_size, HEAD_DIM).transpose(1, 0, 2, 3)
    result = result.reshape(block_rows, heads_kv * group_size * HEAD_DIM)
    return lax.all_to_all(result, "uly", split_axis=0, concat_axis=1, tiled=True)


def solution(mesh):
    in_specs = (P(("blk", "uly"), None), P(("blk", "uly"), None), P(("blk", "uly"), None), P())
    out_specs = P(("blk", "uly"), None)
    return jax.shard_map(local, mesh=mesh, in_specs=in_specs, out_specs=out_specs, check_vma=False)
```

profile of v0, /device:TPU:513, one launch (start us, length us, event | category | flops | bytes accessed | tf_op | source)
XLA Modules:
  0.0 70.9 jit_solution(12808701564459936014)
XLA Ops:
  0.0 1.7 %copy.112 = bf16[12,2,8,512]{3,2,0,1:T(8,128)(2,1)} copy(bf16[12,2,8,512]{3,2,1,0:T(8,128)(2,1)} %bitcast.93) | data formatting | bytes 393216 | tf_op jit(solution)/shard_map/all_to_all | solution.py:52
  1.7 4.1 %all-to-all-start.1 = ((bf16[96,2,512]{2,0,1:T(8,128)(2,1)}), bf16[96,2,512]{2,0,1:T(8,128)(2,1)S(1)}, u32[]{:S(2)}, u32[]{:S(2)}) async-start(bf16[96,2,512]{2,0,1:T(8,128)(2,1)} %bitcast.78), calls=%async_computation.1 | async-start | bytes 393216 | tf_op jit(solution)/shard_map/all_to_all | solution.py:52
  5.8 0.9 %copy.111 = bf16[12,2,8,512]{3,2,0,1:T(8,128)(2,1)S(1)} copy(bf16[12,2,8,512]{3,2,1,0:T(8,128)(2,1)} %bitcast.94) | data formatting | bytes 393216 | tf_op jit(solution)/shard_map/all_to_all | solution.py:53
  6.8 0.2 all-to-all-done.1
  7.0 3.9 %all_to_all.67 = bf16[96,2,512]{2,0,1:T(8,128)(2,1)S(1)} all-to-all(bf16[96,2,512]{2,0,1:T(8,128)(2,1)S(1)} %bitcast.92), channel_id=1, replica_groups=mesh['blk'=512,'uly'=2] {'uly'}, dimensions={1} | all-to-all | bytes 393216 | tf_op jit(solution)/shard_map/all_to_all | solution.py:53
  10.9 0.8 %pad_maximum_fusion = bf16[2,192,512]{2,1,0:T(8,128)(2,1)} fusion(bf16[1,192,512]{2,1,0:T(8,128)(2,1)S(1)} %bitcast.84, bf16[1,192,512]{2,1,0:T(8,128)(2,1)S(1)} %bitcast.86), kind=kLoop, calls=%fused_computation.42 | loop fusion | flops 196608 | bytes 786432 | tf_op jit(solution)/shard_map/stack | solution.py:67
  11.7 4.0 %collective-permute-start.1 = (bf16[2,192,512]{2,1,0:T(8,128)(2,1)}, bf16[2,192,512]{2,1,0:T(8,128)(2,1)}, u32[]{:S(2)}, u32[]{:S(2)}) collective-permute-start(bf16[2,192,512]{2,1,0:T(8,128)(2,1)} %pad_maximum_fusion), channel_id=1, source_target_pairs={{0,4},{2,6},{4,8},{6,10},{8,12},{10,14},{12,16},{14,18},{16,20},{1... | collective-permute-start | bytes 1179656 | tf_op jit(solution)/shard_map/ppermute | solution.py:18
  15.7 3.1 %collective-permute-start = (bf16[2,192,512]{2,1,0:T(8,128)(2,1)}, bf16[2,192,512]{2,1,0:T(8,128)(2,1)}, u32[]{:S(2)}, u32[]{:S(2)}) collective-permute-start(bf16[2,192,512]{2,1,0:T(8,128)(2,1)} %pad_maximum_fusion), channel_id=1, source_target_pairs={{0,2},{2,4},{4,6},{6,8},{8,10},{10,12},{12,14},{14,16},{16,18},{18... | collective-permute-start | bytes 1179656 | tf_op jit(solution)/shard_map/ppermute | solution.py:18
  18.8 0.0 copy-done
  18.8 0.0 copy-start.3
  18.9 1.2 %copy.109 = bf16[12,2,8,4096]{3,2,0,1:T(8,128)(2,1)} copy(bf16[12,2,8,4096]{3,2,1,0:T(8,128)(2,1)S(1)} %bitcast.88) | data formatting | bytes 3145728 | tf_op jit(solution)/shard_map/all_to_all | solution.py:51
  20.1 4.6 %all-to-all-start = ((bf16[96,2,4096]{2,0,1:T(8,128)(2,1)}), bf16[96,2,4096]{2,0,1:T(8,128)(2,1)S(1)}, u32[]{:S(2)}, u32[]{:S(2)}) async-start(bf16[96,2,4096]{2,0,1:T(8,128)(2,1)} %bitcast.75), calls=%async_computation | async-start | bytes 3145728 | tf_op jit(solution)/shard_map/all_to_all | solution.py:51
  24.7 0.0 copy-start.6
  24.7 0.0 copy-start.8
  24.8 0.0 copy-done.3
  24.8 0.3 reduce-window.9
  25.0 0.1 slice.19
  25.1 0.1 slice_reduce_fusion
  25.3 0.1 bitcast_subtract_fusion
  25.3 1.0 %convert_reduce_fusion.3 = (s32[192]{0:T(256)S(1)}, s32[192]{0:T(256)}, s32[192]{0:T(256)}) fusion(s32[1024]{0:T(1024)S(1)} %bitcast_subtract_fusion, s32[192]{0:T(256)S(1)} %iota_add_fusion.2, s32[192]{0:T(256)S(1)} %iota_add_fusion.1, s32[192]{0:T(256)S(1)} %iota_add_fusion), kind=kLoop, calls=%fused_computation.41 | loop fusion | flops 1768896 | bytes 8704 | tf_op jit(solution)/shard_map/reduce_sum | solution.py:22
  26.3 0.5 broadcast_add_fusion.3
  26.8 0.8 %convert_reduce_fusion = s32[1536]{0:T(1024)S(1)} fusion(s32[1024]{0:T(1024)S(1)} %bitcast_subtract_fusion, s32[1536]{0:T(1024)S(1)} %fusion.40), kind=kLoop, calls=%fused_computation | loop fusion | flops 4717056 | bytes 16384 | tf_op jit(solution)/shard_map/reduce_sum | solution.py:22
  27.6 0.1 reshape.319
  27.7 0.0 all-to-all-done
  27.7 0.0 copy-done.4
  27.7 0.0 copy-done.6
  27.7 0.0 copy-done.8
  27.7 0.0 copy-start.11
  27.7 0.0 copy-start.12
  27.7 0.0 copy-start.10
  27.7 0.0 copy-start.5
  27.8 0.0 copy-start.7
  27.8 0.0 copy-start.9
  27.8 0.3 copy.56
  28.1 0.3 copy-done.11
  28.4 0.0 copy-done.12
  28.4 0.0 copy-done.10
  28.4 0.0 copy-done.5
  28.4 0.0 copy-done.7
  28.4 1.4 %compare_and_fusion.2 = (pred[1536,192]{0,1:T(8,128)(4,1)S(1)}, pred[1536,192]{0,1:T(8,128)(4,1)S(1)}, pred[1536,192]{0,1:T(8,128)(4,1)}) fusion(s32[1536]{0:T(1024)S(1)} %fusion.40, s32[1536]{0:T(1024)S(1)} %broadcast_add_fusion, s32[192]{0:T(256)S(1)} %copy-done.5, s32[192]{0:T(256)S(1)} %copy-done.10, s32[192]{0:T(256)S(1)} %copy-done.7, ...), kind=kLoop, calls=%fused_computation.38 | loop fusion | flops 2654208 | bytes 901632 | tf_op jit(solution)/shard_map/and | solution.py:30
  29.9 3.9 %fusion = (f32[4,1536]{1,0:T(4,128)}, f32[4,1536,192]{1,2,0:T(8,128)}) fusion(pred[1536,192]{0,1:T(8,128)(4,1)S(1)} %get-tuple-element.19, bf16[192,4,128]{2,1,0:T(4,128)(2,1)S(1)} %reshape.319, bf16[4,192,8,128]{3,2,0,1:T(8,128)(2,1)S(1)} %bitcast.89), kind=kOutput, calls=%fused_computation.7 | convolution fusion | flops 305522688 | bytes 6807552 | tf_op jit(solution)/shard_map/gqd,gkd->gqk/dot_general | solution.py:34
  33.8 0.1 reshape.320
  33.8 0.0 collective-permute-done.1
  33.8 1.0 %fusion.49 = (bf16[1,192,512]{2,1,0:T(8,128)(2,1)S(1)}, bf16[1,192,512]{2,1,0:T(8,128)(2,1)S(1)}) fusion(bf16[2,192,512]{2,1,0:T(8,128)(2,1)} %collective-permute-done.1), kind=kLoop, calls=%fused_computation.83 | loop fusion | bytes 786432 | tf_op jit(solution)/shard_map/slice | solution.py:81
  34.9 0.1 reshape_squeeze.15
  34.9 0.7 %reshape_squeeze.14 = bf16[192,4,128]{2,1,0:T(4,128)(2,1)} reshape(bf16[1,192,512]{2,1,0:T(8,128)(2,1)S(1)} %get-tuple-element.14) | data formatting | bytes 393216 | tf_op jit(solution)/shard_map/reshape;squeeze | solution.py:32
  35.7 12.4 %collective-permute-done = bf16[2,192,512]{2,1,0:T(8,128)(2,1)} collective-permute-done((bf16[2,192,512]{2,1,0:T(8,128)(2,1)}, bf16[2,192,512]{2,1,0:T(8,128)(2,1)}, u32[]{:S(2)}, u32[]{:S(2)}) %collective-permute-start) | collective-permute-done | bytes 393248 | tf_op jit(solution)/shard_map/ppermute | solution.py:18
  48.1 1.0 %fusion.50 = (bf16[1,192,512]{2,1,0:T(8,128)(2,1)S(1)}, bf16[1,192,512]{2,1,0:T(8,128)(2,1)S(1)}) fusion(bf16[2,192,512]{2,1,0:T(8,128)(2,1)} %collective-permute-done), kind=kLoop, calls=%fused_computation.84 | loop fusion | bytes 786432 | tf_op jit(solution)/shard_map/slice | solution.py:81
  49.2 0.1 reshape_squeeze.13
  49.2 0.0 slice-start
  49.2 0.7 %reshape_squeeze.12 = bf16[192,4,128]{2,1,0:T(4,128)(2,1)} reshape(bf16[1,192,512]{2,1,0:T(8,128)(2,1)S(1)} %get-tuple-element.16) | data formatting | bytes 393216 | tf_op jit(solution)/shard_map/reshape;squeeze | solution.py:32
  49.9 2.4 %fusion.51 = (f32[4,1536]{1,0:T(4,128)S(1)}, f32[4,1536,192]{1,2,0:T(8,128)S(1)}) fusion(bf16[4,192,8,128]{3,2,0,1:T(8,128)(2,1)S(1)} %bitcast.90, bf16[192,4,128]{2,1,0:T(4,128)(2,1)} %reshape_squeeze.14, pred[1536,192]{0,1:T(8,128)(4,1)} %get-tuple-element.21), kind=kOutput, calls=%fused_computation.85 | convolution fusion | flops 305522688 | bytes 6807552 | tf_op jit(solution)/shard_map/gqd,gkd->gqk/dot_general | solution.py:34
  52.3 1.2 %fusion.52 = (f32[4,1536]{1,0:T(4,128)S(1)}, f32[4,1536,192]{1,2,0:T(8,128)S(1)}) fusion(bf16[4,192,8,128]{3,2,0,1:T(8,128)(2,1)S(1)} %bitcast.91, bf16[192,4,128]{2,1,0:T(4,128)(2,1)S(1)} %copy-done.1, pred[1536,192]{0,1:T(8,128)(4,1)S(1)} %get-tuple-element.20), kind=kOutput, calls=%fused_computation.86 | convolution fusion | flops 305522688 | bytes 6807552 | tf_op jit(solution)/shard_map/gqd,gkd->gqk/dot_general | solution.py:34
  53.5 0.0 copy-done.2
  53.6 1.1 %fusion.5 = f32[4,1536]{1,0:T(4,128)S(1)} fusion(f32[4,1536,192]{1,2,0:T(8,128)S(1)} %bitcast.83, f32[4,1536]{1,0:T(4,128)S(1)} %get-tuple-element.18, pred[1536,192]{0,1:T(8,128)(4,1)S(1)} %get-tuple-element.19), kind=kLoop, calls=%fused_computation.12 | loop fusion | flops 4712448 | bytes 5062656 | tf_op jit(solution)/shard_map/reduce_sum | solution.py:41
  54.7 0.7 fusion.3
  55.3 0.7 fusion.1
  56.1 3.1 %fusion.7 = f32[4,1536,128]{2,1,0:T(8,128)S(1)} fusion(f32[4,1536,192]{1,2,0:T(8,128)S(1)} %bitcast.83, f32[4,1536]{1,0:T(4,128)S(1)} %get-tuple-element.18, pred[1536,192]{0,1:T(8,128)(4,1)S(1)} %get-tuple-element.19, f32[4,1536]{1,0:T(4,128)S(1)} %get-tuple-element.9, f32[4,1536]{1,0:T(4,128)S(1)} %get-tuple-element.17, bf16[192,4,128]{2,1,0:T(4,128)(2,1)S(1)} %reshape.320), kind=kOutput, calls=%fused_computation.17 | convolution fusion | flops 308281344 | bytes 8429568 | tf_op jit(solution)/shard_map/gqk,gkd->gqd/dot_general | solution.py:43
  59.2 2.2 %fusion.8 = f32[4,1536,128]{2,1,0:T(8,128)S(1)} fusion(f32[4,1536,128]{2,1,0:T(8,128)S(1)} %fusion.7, f32[4,1536,192]{1,2,0:T(8,128)S(1)} %get-tuple-element.25, f32[4,1536]{1,0:T(4,128)S(1)} %get-tuple-element.12, f32[4,1536]{1,0:T(4,128)S(1)} %get-tuple-element.10, bf16[192,4,128]{2,1,0:T(4,128)(2,1)S(1)} %reshape_squeeze.13), kind=kOutput, calls=%fused_computation.18 | convolution fusion | flops 305922048 | bytes 11255808 | tf_op jit(solution)/shard_map/gqk,gkd->gqd/dot_general | solution.py:43
  61.4 2.1 %fusion.22 = bf16[4,192,8,128]{3,2,1,0:T(8,128)(2,1)S(1)} fusion(f32[4,1536]{1,0:T(4,128)S(1)} %get-tuple-element.8, f32[4,1536,128]{2,1,0:T(8,128)S(1)} %fusion.8, f32[4,1536,192]{1,2,0:T(8,128)S(1)} %get-tuple-element.23, f32[4,1536]{1,0:T(4,128)S(1)} %get-tuple-element.11, bf16[192,4,128]{2,1,0:T(4,128)(2,1)S(1)} %reshape_squeeze.15), kind=kOutput, calls=%fused_computation.32 | convolution fusion | flops 306708480 | bytes 9682944 | tf_op jit(solution)/shard_map/gqk,gkd->gqd/dot_general | solution.py:43
  63.5 0.3 copy.110
  63.8 0.7 %all_to_all.59 = bf16[2,96,4096]{2,1,0:T(8,128)(2,1)S(1)} reshape(bf16[192,4,8,128]{3,2,1,0:T(8,128)(2,1)S(1)} %bitcast.80) | data formatting | bytes 3145728 | tf_op jit(solution)/shard_map/all_to_all | solution.py:86
  64.6 5.1 %all_to_all.68 = bf16[2,96,4096]{2,1,0:T(8,128)(2,1)S(1)} all-to-all(bf16[2,96,4096]{2,1,0:T(8,128)(2,1)S(1)} %all_to_all.59), channel_id=1, replica_groups=mesh['blk'=512,'uly'=2] {'uly'}, dimensions={0} | all-to-all | bytes 3145728 | tf_op jit(solution)/shard_map/all_to_all | solution.py:86
  69.7 1.2 %copy.55 = bf16[2,12,8,4096]{3,2,0,1:T(8,128)(2,1)} copy(bf16[2,12,8,4096]{3,2,1,0:T(8,128)(2,1)S(1)} %bitcast.81) | data formatting | bytes 3145728 | tf_op jit(solution)/shard_map/all_to_all | solution.py:86
  (19 shorter events, 0.1 us)
Async XLA Ops:
  0.0 18.8 %copy-start = (bf16[96,8192]{1,0:T(8,128)(2,1)S(1)}, bf16[96,8192]{1,0:T(8,128)(2,1)}, u32[]{:S(2)}) copy-start(bf16[96,8192]{1,0:T(8,128)(2,1)} %param.4) | copy-start | bytes 4718596
  1.7 5.3 %all-to-all-start.1 = ((bf16[96,2,512]{2,0,1:T(8,128)(2,1)}), bf16[96,2,512]{2,0,1:T(8,128)(2,1)S(1)}, u32[]{:S(2)}, u32[]{:S(2)}) async-start(bf16[96,2,512]{2,0,1:T(8,128)(2,1)} %bitcast.78), calls=%async_computation.1 | async-start | bytes 393216 | tf_op jit(solution)/shard_map/all_to_all | solution.py:52
  11.7 22.1 %collective-permute-start.1 = (bf16[2,192,512]{2,1,0:T(8,128)(2,1)}, bf16[2,192,512]{2,1,0:T(8,128)(2,1)}, u32[]{:S(2)}, u32[]{:S(2)}) collective-permute-start(bf16[2,192,512]{2,1,0:T(8,128)(2,1)} %pad_maximum_fusion), channel_id=1, source_target_pairs={{0,4},{2,6},{4,8},{6,10},{8,12},{10,14},{12,16},{14,18},{16,20},{1... | collective-permute-start | bytes 1179656 | tf_op jit(solution)/shard_map/ppermute | solution.py:18
  15.7 32.4 %collective-permute-start = (bf16[2,192,512]{2,1,0:T(8,128)(2,1)}, bf16[2,192,512]{2,1,0:T(8,128)(2,1)}, u32[]{:S(2)}, u32[]{:S(2)}) collective-permute-start(bf16[2,192,512]{2,1,0:T(8,128)(2,1)} %pad_maximum_fusion), channel_id=1, source_target_pairs={{0,2},{2,4},{4,6},{6,8},{8,10},{10,12},{12,14},{14,16},{16,18},{18... | collective-permute-start | bytes 1179656 | tf_op jit(solution)/shard_map/ppermute | solution.py:18
  18.8 5.9 %copy-start.3 = (s32[1024]{0:T(1024)S(1)}, s32[1024]{0:T(1024)}, u32[]{:S(2)}) copy-start(s32[1024]{0:T(1024)} %param.7) | copy-start | bytes 12292
  20.1 7.6 %all-to-all-start = ((bf16[96,2,4096]{2,0,1:T(8,128)(2,1)}), bf16[96,2,4096]{2,0,1:T(8,128)(2,1)S(1)}, u32[]{:S(2)}, u32[]{:S(2)}) async-start(bf16[96,2,4096]{2,0,1:T(8,128)(2,1)} %bitcast.75), calls=%async_computation | async-start | bytes 3145728 | tf_op jit(solution)/shard_map/all_to_all | solution.py:51
  24.7 3.0 %copy-start.4 = (s32[192]{0:T(256)}, s32[192]{0:T(256)S(1)}, u32[]{:S(2)}) copy-start(s32[192]{0:T(256)S(1)} %iota_add_fusion.2) | copy-start | bytes 2308
  24.7 3.0 %copy-start.6 = (s32[192]{0:T(256)}, s32[192]{0:T(256)S(1)}, u32[]{:S(2)}) copy-start(s32[192]{0:T(256)S(1)} %iota_add_fusion.1) | copy-start | bytes 2308
  24.7 3.0 %copy-start.8 = (s32[192]{0:T(256)}, s32[192]{0:T(256)S(1)}, u32[]{:S(2)}) copy-start(s32[192]{0:T(256)S(1)} %iota_add_fusion) | copy-start | bytes 2308
  27.7 0.7 copy-start.11
  27.7 0.7 copy-start.12
  27.7 0.7 copy-start.10
  27.7 0.7 copy-start.5
  27.8 0.7 copy-start.7
  27.8 0.7 copy-start.9
  49.2 4.4 %slice-start = ((s8[4718592]{0:T(1024)(128)(4,1)}), s8[524288]{0:T(1024)(128)(4,1)S(1)}, s32[]{:S(2)}) async-start(s8[4718592]{0:T(1024)(128)(4,1)} %bitcast.82), calls=%async_computation.4 | async-start | bytes 1048576
  49.9 2.4 %copy-start.1 = (bf16[192,4,128]{2,1,0:T(4,128)(2,1)S(1)}, bf16[192,4,128]{2,1,0:T(4,128)(2,1)}, u32[]{:S(2)}) copy-start(bf16[192,4,128]{2,1,0:T(4,128)(2,1)} %reshape_squeeze.12) | copy-start | bytes 589828
  49.9 3.6 %slice-start.1 = ((s8[4718592]{0:T(1024)(128)(4,1)}), s8[4194304]{0:T(1024)(128)(4,1)S(1)}, s32[]{:S(2)}) async-start(s8[4718592]{0:T(1024)(128)(4,1)} %bitcast.82), calls=%async_computation.5 | async-start | bytes 8388608
  52.3 1.2 %copy-start.2 = (f32[4,1536]{1,0:T(4,128)S(1)}, f32[4,1536]{1,0:T(4,128)}, u32[]{:S(2)}) copy-start(f32[4,1536]{1,0:T(4,128)} %get-tuple-element.26) | copy-start | bytes 73732
where the time goes:
time: 71.4 us; the launch traced here: 70.9 us
  starting transfers between devices  15.8 us (22%)
  matrix products  14.9 us (21%)
  waiting for transfers between devices  12.7 us (18%)
  local copies, waits for them, and re-layouts  10.8 us (15%)
  blocking collectives  8.97 us (13%)
  other arithmetic  7.37 us (10%)
    ppermute x2, waiting for transfers between devices, from_behind(): return lax.ppermute(value, axis, pairs)  12.4 us
    dot_general x3, matrix products, fold_block(): jnp.einsum('gqk,gkd->gqd', rounded, value_heads, preferred_element_type=j...  7.46 us
    dot_general x3, matrix products, fold_block(): jnp.einsum('gqd,gkd->gqk', grouped, key_heads, preferred_element_type=jnp...  7.45 us
    ppermute x2, starting transfers between devices, from_behind(): return lax.ppermute(value, axis, pairs)  7.16 us
    all_to_all x1, blocking collectives, local(): lax.all_to_all(result, 'uly', split_axis=0, concat_axis=1, tiled=True)  5.1 us
    all_to_all x1, starting transfers between devices, local(): lax.all_to_all(queries, 'uly', split_axis=1, concat_axis=0, tiled=True)  4.58 us
    all_to_all x1, starting transfers between devices, local(): lax.all_to_all(keys, 'uly', split_axis=1, concat_axis=0, tiled=True)  4.1 us
    all_to_all x1, blocking collectives, local(): lax.all_to_all(values, 'uly', split_axis=1, concat_axis=0, tiled=True)  3.88 us
  transfers between devices with their start and end apart: 4, of which 2 were waited for; matrix products, arithmetic and copies ran while one was open for 18% of the time, Pallas kernels for 0%

commit v1 on v0

v1 whole, which is shorter than its diff:
```python
import functools

import jax
import jax.numpy as jnp
from jax import lax
from jax.experimental import pallas as pl
from jax.experimental.pallas import tpu as pltpu
from jax.sharding import PartitionSpec as P

KV_HEADS = 8
GROUP = 8
JOINED = 4
HEAD_DIM = 128
TOK = 96
WIDE = GROUP * HEAD_DIM
PAD = 512
OWN = 4 * TOK
MASKED = -1e30
REACH = 2
COPIES = REACH * KV_HEADS
WINDOW = 4
LAG = 3
MESH = pl.DeviceIdType.MESH
EXP_SCALE = (HEAD_DIM ** -0.5) * 1.4426950408889634


def prefix_starts(lengths):
    lane = lax.broadcasted_iota(jnp.int32, lengths.shape, 1)
    row = lax.broadcasted_iota(jnp.int32, lengths.shape, 0)
    run = lengths
    shift = 1
    while shift < 128:
        run = run + jnp.where(lane >= shift, pltpu.roll(run, shift, 1), 0)
        shift *= 2
    totals = jnp.broadcast_to(jnp.sum(lengths, axis=1, keepdims=True), lengths.shape)
    base = jnp.zeros_like(lengths)
    for j in range(7):
        base = base + jnp.where(row > j, totals[j:j + 1, :], 0)
    return base + run - lengths


def fill_bias(lengths, me, bias):
    starts = prefix_starts(lengths)
    token = lax.broadcasted_iota(jnp.int32, (TOK, 128), 0) + me * TOK
    begin = jnp.zeros((TOK, 128), jnp.int32)
    for j in range(8):
        begin = jnp.maximum(begin, jnp.where(starts[j:j + 1, :] <= token, starts[j:j + 1, :], 0))
    begin = jnp.max(begin, axis=1, keepdims=True)
    key = lax.broadcasted_iota(jnp.int32, (TOK, PAD), 1) + (me - 4) * TOK
    query = lax.broadcasted_iota(jnp.int32, (TOK, PAD), 0) + me * TOK
    bias[...] = jnp.where((key >= begin) & (key <= query), 0.0, MASKED).astype(jnp.float32)


def attend(q, k, v, bias):
    scores = lax.dot_general(q, k, (((1,), (1,)), ((), ())), preferred_element_type=jnp.float32)
    scores = scores + bias
    top = jnp.max(scores, axis=1, keepdims=True)
    weights = jnp.exp2((scores - top) * EXP_SCALE)
    total = jnp.sum(weights, axis=1, keepdims=True)
    acc = jnp.dot(weights.astype(jnp.bfloat16), v, preferred_element_type=jnp.float32)
    return (acc / total).astype(jnp.bfloat16)


def kernel(n, doc_hbm, q_hbm, k_hbm, v_hbm, o_ref, docs, qbuf, kv, bias,
           doc_sem, q_sem, load_sem, send, recv, send_p, recv_p, send_r, recv_r):
    c = lax.axis_index("blk")
    core = lax.axis_index("uly")
    me = c * 2 + core

    def load(h, which, src):
        return pltpu.make_async_copy(
            src.at[:, h * HEAD_DIM:(h + 1) * HEAD_DIM], kv.at[h, which, pl.ds(OWN, TOK)], load_sem.at[h, which])

    for h in range(KV_HEADS):
        load(h, 0, k_hbm).start()
        load(h, 1, v_hbm).start()
    doc_copy = pltpu.make_async_copy(doc_hbm, docs, doc_sem)
    doc_copy.start()
    q_copy = pltpu.make_async_copy(q_hbm, qbuf, q_sem)
    q_copy.start()

    @pl.when(c < REACH)
    def _():
        for h in range(KV_HEADS):
            kv[h, :, :OWN, :] = jnp.zeros((2, OWN, HEAD_DIM), jnp.bfloat16)

    barrier = pltpu.get_barrier_semaphore()

    def greet(target):
        pl.semaphore_signal(barrier, inc=1, device_id=target, device_id_type=MESH)

    @pl.when(c > 0)
    def _():
        greet((c - 1, core))

    @pl.when(c < n - 1)
    def _():
        greet((c + 1, core))

    greet((c, 1 - core))
    pl.semaphore_wait(barrier, 1 + jnp.where(c > 0, 1, 0) + jnp.where(c < n - 1, 1, 0))

    def remote(h, src_row, dst_row, send_sem, recv_sem, target):
        return pltpu.make_async_remote_copy(
            src_ref=kv.at[h, :, pl.ds(src_row, TOK)], dst_ref=kv.at[h, :, pl.ds(dst_row, TOK)],
            send_sem=send_sem, recv_sem=recv_sem, device_id=target, device_id_type=MESH)

    def ahead(i):
        lap = i // KV_HEADS
        return remote(i % KV_HEADS, pl.multiple_of(OWN - 2 * TOK * lap, TOK), pl.multiple_of(2 * TOK - 2 * TOK * lap, TOK),
                      send.at[i], recv.at[i], (c + 1, core))

    def sends(i):
        return (c < n - 1) & (c >= i // KV_HEADS)

    def receives(i):
        return c >= 1 + i // KV_HEADS

    def partner_near(h):
        return remote(h, pl.multiple_of(OWN - 2 * TOK * core, TOK), 3 * TOK, send_p.at[h], recv_p.at[h], (c, 1 - core))

    def partner_far(h):
        return remote(h, pl.multiple_of(2 * TOK - 2 * TOK * core, TOK), TOK, send_r.at[h], recv_r.at[h], (c, 1 - core))

    for h in range(KV_HEADS):
        load(h, 0, k_hbm).wait()
        load(h, 1, v_hbm).wait()
        if h < WINDOW:
            @pl.when(sends(h))
            def _(h=h):
                ahead(h).start()

    for h in range(KV_HEADS):
        kv[h, :, 5 * TOK:, :] = jnp.zeros((2, PAD - 5 * TOK, HEAD_DIM), jnp.bfloat16)
    doc_copy.wait()
    fill_bias(docs[...], me, bias)
    q_copy.wait()

    def step(i, carry):
        @pl.when((i < COPIES) & sends(i))
        def _():
            ahead(i).wait_send()

        @pl.when((i + WINDOW < COPIES) & sends(i + WINDOW))
        def _():
            ahead(i + WINDOW).start()

        j = i - LAG

        @pl.when((j >= 0) & (j < COPIES) & receives(j))
        def _():
            ahead(j).wait_recv()

        @pl.when((j >= 0) & (j < KV_HEADS) & (c >= core))
        def _():
            partner_near(j).start()

        @pl.when((j >= KV_HEADS) & (j < COPIES) & (c >= 1 + core))
        def _():
            partner_far(j - KV_HEADS).start()

        h = i - LAG - 1 - KV_HEADS

        @pl.when(h >= 0)
        def _():
            @pl.when(c >= 1 - core)
            def _():
                partner_near(h).wait_recv()

            @pl.when(c >= 2 - core)
            def _():
                partner_far(h).wait_recv()

            k, v = kv[h, 0], kv[h, 1]
            wide_bias = jnp.concatenate([bias[...]] * JOINED, axis=0)
            for g in range(0, GROUP, JOINED):
                cols = [pl.ds(pl.multiple_of(h * WIDE + (g + t) * HEAD_DIM, HEAD_DIM), HEAD_DIM) for t in range(JOINED)]
                result = attend(jnp.concatenate([qbuf[:, at] for at in cols], axis=0), k, v, wide_bias)
                for t, at in enumerate(cols):
                    o_ref[:, at] = result[t * TOK:(t + 1) * TOK]

            @pl.when(c >= core)
            def _():
                partner_near(h).wait_send()

            @pl.when(c >= 1 + core)
            def _():
                partner_far(h).wait_send()

        return carry

    lax.fori_loop(0, COPIES + LAG + 1, step, 0)


def local(queries, keys, values, doc_lengths):
    n = lax.axis_size("blk")
    hbm = pl.BlockSpec(memory_space=pltpu.HBM)
    per_head = pltpu.SemaphoreType.DMA((KV_HEADS,))
    return pl.pallas_call(
        functools.partial(kernel, n),
        out_shape=pltpu.VMEM(queries.shape, jnp.bfloat16),
        in_specs=[hbm] * 4,
        out_specs=pl.BlockSpec(memory_space=pltpu.VMEM),
        scratch_shapes=[
            pltpu.VMEM((8, 128), jnp.int32),
            pltpu.VMEM(queries.shape, jnp.bfloat16),
            pltpu.VMEM((KV_HEADS, 2, PAD, HEAD_DIM), jnp.bfloat16),
            pltpu.VMEM((TOK, PAD), jnp.float32),
            pltpu.SemaphoreType.DMA,
            pltpu.SemaphoreType.DMA,
            pltpu.SemaphoreType.DMA((KV_HEADS, 2)),
        ] + [pltpu.SemaphoreType.DMA((COPIES,))] * 2 + [per_head] * 4,
        compiler_params=pltpu.CompilerParams(
            collective_id=0, has_side_effects=True, vmem_limit_bytes=32 * 1024 * 1024),
    )(*[pltpu.with_memory_space_constraint(x, pltpu.HBM) for x in (doc_lengths.reshape(8, 128), queries, keys, values)])


def solution(mesh):
    in_specs = (P(("blk", "uly"), None), P(("blk", "uly"), None), P(("blk", "uly"), None), P())
    out_specs = P(("blk", "uly"), None)
    return jax.shard_map(local, mesh=mesh, in_specs=in_specs, out_specs=out_specs, check_vma=False)
```

time: 71.4 us -> 40.3 us (0.56)
  the two profiles are of different devices: /device:TPU:513 before, /device:TPU:831 now
where the time goes in v1:
time: 40.3 us; the launch traced here: 40.1 us
  Pallas kernels  39 us (97%)
  local copies, waits for them, and re-layouts  1.15 us (3%)
    pallas_call x1, Pallas kernels, local(): pl.pallas_call(functools.partial(kernel, n), out_shape=pltpu.VMEM(queries...  39 us
    unnamed x1, local copies, waits for them, and re-layouts  1.15 us

profile of v1, /device:TPU:831, one launch (start us, length us, event | category | flops | bytes accessed | tf_op | source)
XLA Modules:
  0.0 40.1 jit_solution(1934151688899344725)
XLA Ops:
  0.0 39.0 %shard_map.46 = bf16[96,8192]{1,0:T(8,128)(2,1)S(1)} custom-call(s32[8,128]{1,0:T(8,128)} %bitcast.1, bf16[96,8192]{1,0:T(8,128)(2,1)} %q_hbm.1, bf16[96,1024]{1,0:T(8,128)(2,1)} %k_hbm.1, bf16[96,1024]{1,0:T(8,128)(2,1)} %v_hbm.1), custom_call_target="tpu_custom_call" | custom-call | tf_op jit(solution)/shard_map/pallas_call | solution.py:199
  39.0 1.1 %copy.6 = bf16[96,8192]{1,0:T(8,128)(2,1)} copy(bf16[96,8192]{1,0:T(8,128)(2,1)S(1)} %shard_map.46) | data formatting | bytes 3145728

commit v2 on v1

v2 whole, which is shorter than its diff:
```python
import functools

import jax
import jax.numpy as jnp
from jax import lax
from jax.experimental import pallas as pl
from jax.experimental.pallas import tpu as pltpu
from jax.sharding import PartitionSpec as P

KV_HEADS = 8
GROUP = 8
JOINED = 4
HEAD_DIM = 128
TOK = 96
WIDE = GROUP * HEAD_DIM
PAD = 32
WINDOW = 512
HALF = WINDOW // 2
OWN = PAD + 4 * TOK
MASKED = -1e30
REACH = 2
COPIES = REACH * KV_HEADS
ROW = 8
PLANE = 8 * ROW
MESH = pl.DeviceIdType.MESH
EXP_SCALE = (HEAD_DIM ** -0.5) * 1.4426950408889634


def prefix_starts(lengths):
    lane = lax.broadcasted_iota(jnp.int32, lengths.shape, 1)
    row = lax.broadcasted_iota(jnp.int32, lengths.shape, 0)
    run = lengths
    shift = 1
    while shift < 128:
        run = run + jnp.where(lane >= shift, pltpu.roll(run, shift, 1), 0)
        shift *= 2
    totals = jnp.broadcast_to(jnp.sum(lengths, axis=1, keepdims=True), lengths.shape)
    base = jnp.zeros_like(lengths)
    for j in range(7):
        base = base + jnp.where(row > j, totals[j:j + 1, :], 0)
    return base + run - lengths


def fill_bias(lengths, me, bias):
    starts = prefix_starts(lengths)
    token = lax.broadcasted_iota(jnp.int32, (TOK, 128), 0) + me * TOK
    begin = jnp.zeros((TOK, 128), jnp.int32)
    for j in range(8):
        begin = jnp.maximum(begin, jnp.where(starts[j:j + 1, :] <= token, starts[j:j + 1, :], 0))
    begin = jnp.max(begin, axis=1, keepdims=True)
    place = lax.broadcasted_iota(jnp.int32, (TOK, WINDOW), 1)
    key = place + (me * TOK - OWN)
    query = lax.broadcasted_iota(jnp.int32, (TOK, WINDOW), 0) + me * TOK
    bias[...] = jnp.where((place >= PAD) & (key >= begin) & (key <= query), 0.0, MASKED).astype(jnp.float32)


def twice(x):
    return jnp.concatenate([x, x], axis=1)


def masked_scores(q, k, bias):
    scores = lax.dot_general(q, k, (((1,), (1,)), ((), ())), preferred_element_type=jnp.float32)
    return scores + jnp.concatenate([bias] * JOINED, axis=0)


def row_max(scores):
    return jnp.broadcast_to(jnp.max(scores, axis=1, keepdims=True), (scores.shape[0], HEAD_DIM))


def weighted(scores, top, v):
    weights = jnp.exp2((scores - twice(top)) * EXP_SCALE)
    return jnp.dot(weights.astype(jnp.bfloat16), v, preferred_element_type=jnp.float32)


def with_ones(v):
    return jnp.concatenate([v, jnp.ones_like(v)], axis=1)


def kernel(n, doc_hbm, q_hbm, k_hbm, v_hbm, o_ref, docs, qbuf, kv, held, bias, sums, tops,
           doc_sem, q_sem, load_sem, send, recv, relay_out, relay_in, send_p, recv_p, send_r, recv_r):
    c = lax.axis_index("blk")
    core = lax.axis_index("uly")
    me = c * 2 + core
    relays = (c % ROW == ROW - 1) & (c < PLANE)
    origin = jnp.where(c < ROW, PLANE - 1, c - ROW)
    relay = jnp.where(c < PLANE - ROW, c + ROW, ROW - 1)
    relayed = (c % ROW == 0) & (c > 0) & (c <= PLANE)
    before = jnp.where(relayed, jnp.where(c < PLANE, c + ROW - 1, ROW - 1), c - 1)
    has_next = c < n - 1

    def load(h, which, src):
        return pltpu.make_async_copy(
            src.at[:, h * HEAD_DIM:(h + 1) * HEAD_DIM], kv.at[h, which, pl.ds(OWN, TOK)], load_sem.at[h, which])

    for h in range(KV_HEADS):
        load(h, 0, k_hbm).start()
        load(h, 1, v_hbm).start()
    doc_copy = pltpu.make_async_copy(doc_hbm, docs, doc_sem)
    doc_copy.start()
    q_copy = pltpu.make_async_copy(q_hbm, qbuf, q_sem)
    q_copy.start()

    @pl.when(c < REACH)
    def _():
        for h in range(KV_HEADS):
            kv[h, :, PAD:OWN, :] = jnp.zeros((2, OWN - PAD, HEAD_DIM), jnp.bfloat16)

    barrier = pltpu.get_barrier_semaphore()

    def greet(target):
        pl.semaphore_signal(barrier, inc=1, device_id=target, device_id_type=MESH)

    @pl.when(c > 0)
    def _():
        greet((before, core))

    @pl.when(relays)
    def _():
        greet((origin, core))

    @pl.when(c >= 1 - core)
    def _():
        greet((c, 1 - core))

    pl.semaphore_wait(
        barrier, jnp.where(c >= core, 1, 0) + jnp.where(has_next, 1, 0) + jnp.where(relays, 1, 0))

    def remote(src, dst, send_sem, recv_sem, target):
        return pltpu.make_async_remote_copy(
            src_ref=src, dst_ref=dst, send_sem=send_sem, recv_sem=recv_sem, device_id=target, device_id_type=MESH)

    def rows(h, row):
        return kv.at[h, :, pl.ds(row, TOK)]

    def chunk(i):
        lap = i // KV_HEADS
        src = pl.multiple_of(OWN - 2 * TOK * lap, PAD)
        return rows(i % KV_HEADS, src), rows(i % KV_HEADS, pl.multiple_of(src - 2 * TOK, PAD))

    def ahead(i):
        src, dst = chunk(i)
        return remote(src, dst, send.at[i], recv.at[i], (c + 1, core))

    def to_relay(i):
        return remote(chunk(i)[0], held.at[i], send.at[i], relay_in.at[i], (relay, core))

    def from_relay(i):
        return remote(held.at[i], chunk(i)[1], relay_out.at[i], recv.at[i], (origin + 1, core))

    def start_ahead(i):
        @pl.when(jnp.logical_not(relays))
        def _():
            ahead(i).start()

        @pl.when(relays)
        def _():
            to_relay(i).start()

    def across(h, src, dst, send_sem, recv_sem):
        return remote(rows(h, PAD + src * TOK), rows(h, PAD + dst * TOK), send_sem.at[h], recv_sem.at[h], (c, 1 - core))

    def own_across(h):
        return across(h, 4, 3, send_p, recv_p)

    def near_across(h):
        return across(h, 2, 3, send_p, recv_p)

    def mid_across(h):
        return across(h, 2, 1, send_r, recv_r)

    def far_across(h):
        return across(h, 0, 1, send_r, recv_r)

    for h in range(KV_HEADS):
        load(h, 0, k_hbm).wait()
        load(h, 1, v_hbm).wait()

        @pl.when(has_next)
        def _(h=h):
            start_ahead(h)

        @pl.when(core == 0)
        def _(h=h):
            own_across(h).start()

    for h in range(KV_HEADS):
        kv[h, :, :PAD, :] = jnp.zeros((2, PAD, HEAD_DIM), jnp.bfloat16)
    doc_copy.wait()
    fill_bias(docs[...], me, bias)
    q_copy.wait()

    def step(i, carry):
        @pl.when(relays & (i < COPIES))
        def _():
            from_relay_in(i)
            from_relay(i).start()

        @pl.when((c >= 1) & (i < KV_HEADS))
        def _():
            ahead(i).wait_recv()

            @pl.when(has_next)
            def _():
                start_ahead(i + KV_HEADS)

            @pl.when(core == 0)
            def _():
                mid_across(i).start()

            @pl.when(core == 1)
            def _():
                near_across(i).start()

        @pl.when((c >= 2) & (i >= KV_HEADS) & (i < COPIES))
        def _():
            ahead(i).wait_recv()

            @pl.when(core == 1)
            def _():
                far_across(i - KV_HEADS).start()

        @pl.when((i >= 1) & (i <= KV_HEADS))
        def _():
            h = i - 1

            @pl.when(c >= 1 - core)
            def _():
                own_across(h).wait_recv()

            k, v = kv[h, 0, HALF:], with_ones(kv[h, 1, HALF:])
            for g in range(0, GROUP, JOINED):
                scores = masked_scores(joined_queries(h, g), k, bias[:, HALF:])
                top = row_max(scores)
                at = pl.ds(g * TOK, JOINED * TOK)
                tops[h, at, :] = top
                sums[h, at, :] = weighted(scores, top, v)

        @pl.when(i > KV_HEADS)
        def _():
            h = i - 1 - KV_HEADS

            @pl.when(c >= 2 - core)
            def _():
                far_across(h).wait_recv()

            k, v = kv[h, 0, :HALF], with_ones(kv[h, 1, :HALF])
            for g in range(0, GROUP, JOINED):
                scores = masked_scores(joined_queries(h, g), k, bias[:, :HALF])
                at = pl.ds(g * TOK, JOINED * TOK)
                near_top = tops[h, at, :]
                top = jnp.maximum(near_top, row_max(scores))
                rescale = jnp.exp2((near_top - top) * EXP_SCALE)
                total = sums[h, at, :] * twice(rescale) + weighted(scores, top, v)
                result = (total[:, :HEAD_DIM] / total[:, HEAD_DIM:]).astype(jnp.bfloat16)
                for t in range(JOINED):
                    o_ref[:, columns(h, g + t)] = result[t * TOK:(t + 1) * TOK]

        return carry

    def columns(h, g):
        return pl.ds(pl.multiple_of(h * WIDE + g * HEAD_DIM, HEAD_DIM), HEAD_DIM)

    def joined_queries(h, g):
        return jnp.concatenate([qbuf[:, columns(h, g + t)] for t in range(JOINED)], axis=0)

    def from_relay_in(i):
        remote(held.at[i], held.at[i], relay_out.at[i], relay_in.at[i], (origin + 1, core)).wait_recv()

    lax.fori_loop(0, COPIES + 1, step, 0)

    def drain(i, carry):
        @pl.when(has_next & (c >= i // KV_HEADS))
        def _():
            ahead(i).wait_send()

        @pl.when(relays)
        def _():
            from_relay(i).wait_send()

        @pl.when((i < KV_HEADS) & (c >= core))
        def _():
            own_across(i).wait_send()

        @pl.when((i >= KV_HEADS) & (c >= 1 + core))
        def _():
            far_across(i - KV_HEADS).wait_send()

        return carry

    lax.fori_loop(0, COPIES, drain, 0)


def local(queries, keys, values, doc_lengths):
    n = lax.axis_size("blk")
    hbm = pl.BlockSpec(memory_space=pltpu.HBM)
    per_head = pltpu.SemaphoreType.DMA((KV_HEADS,))
    return pl.pallas_call(
        functools.partial(kernel, n),
        out_shape=pltpu.VMEM(queries.shape, jnp.bfloat16),
        in_specs=[hbm] * 4,
        out_specs=pl.BlockSpec(memory_space=pltpu.VMEM),
        scratch_shapes=[
            pltpu.VMEM((8, 128), jnp.int32),
            pltpu.VMEM(queries.shape, jnp.bfloat16),
            pltpu.VMEM((KV_HEADS, 2, WINDOW, HEAD_DIM), jnp.bfloat16),
            pltpu.VMEM((COPIES, 2, TOK, HEAD_DIM), jnp.bfloat16),
            pltpu.VMEM((TOK, WINDOW), jnp.float32),
            pltpu.VMEM((KV_HEADS, GROUP * TOK, 2 * HEAD_DIM), jnp.float32),
            pltpu.VMEM((KV_HEADS, GROUP * TOK, HEAD_DIM), jnp.float32),
            pltpu.SemaphoreType.DMA,
            pltpu.SemaphoreType.DMA,
            pltpu.SemaphoreType.DMA((KV_HEADS, 2)),
        ] + [pltpu.SemaphoreType.DMA((COPIES,))] * 4 + [per_head] * 4,
        compiler_params=pltpu.CompilerParams(
            collective_id=0, has_side_effects=True, vmem_limit_bytes=32 * 1024 * 1024),
    )(*[pltpu.with_memory_space_constraint(x, pltpu.HBM) for x in (doc_lengths.reshape(8, 128), queries, keys, values)])


def solution(mesh):
    in_specs = (P(("blk", "uly"), None), P(("blk", "uly"), None), P(("blk", "uly"), None), P())
    out_specs = P(("blk", "uly"), None)
    return jax.shard_map(local, mesh=mesh, in_specs=in_specs, out_specs=out_specs, check_vma=False)
```

time: 40.3 us -> 30.7 us (0.76)
  the two profiles are of different devices: /device:TPU:831 before, /device:TPU:16 now
where the time goes in v2:
time: 30.7 us; the launch traced here: 30.5 us
  Pallas kernels  29.4 us (96%)
  local copies, waits for them, and re-layouts  1.15 us (4%)
    pallas_call x1, Pallas kernels, local(): pl.pallas_call(functools.partial(kernel, n), out_shape=pltpu.VMEM(queries...  29.4 us
    unnamed x1, local copies, waits for them, and re-layouts  1.15 us

profile of v2, /device:TPU:16, one launch (start us, length us, event | category | flops | bytes accessed | tf_op | source)
XLA Modules:
  0.0 30.5 jit_solution(2196025017482085705)
XLA Ops:
  0.0 29.4 %shard_map.46 = bf16[96,8192]{1,0:T(8,128)(2,1)S(1)} custom-call(s32[8,128]{1,0:T(8,128)} %bitcast.1, bf16[96,8192]{1,0:T(8,128)(2,1)} %q_hbm.1, bf16[96,1024]{1,0:T(8,128)(2,1)} %k_hbm.1, bf16[96,1024]{1,0:T(8,128)(2,1)} %v_hbm.1), custom_call_target="tpu_custom_call" | custom-call | tf_op jit(solution)/shard_map/pallas_call | solution.py:297
  29.4 1.1 %copy.6 = bf16[96,8192]{1,0:T(8,128)(2,1)} copy(bf16[96,8192]{1,0:T(8,128)(2,1)S(1)} %shard_map.46) | data formatting | bytes 3145728

commit v3 on v2

--- a/solution.py
+++ b/solution.py
@@ -142,10 +142,12 @@
         return remote(src, dst, send.at[i], recv.at[i], (c + 1, core))
 
     def to_relay(i):
-        return remote(chunk(i)[0], held.at[i], send.at[i], relay_in.at[i], (relay, core))
+        src = chunk(i)[0]
+        return [remote(src.at[t], held.at[i, t], send.at[i], relay_in.at[i, t], (relay, core)) for t in range(2)]
 
     def from_relay(i):
-        return remote(held.at[i], chunk(i)[1], relay_out.at[i], recv.at[i], (origin + 1, core))
+        dst = chunk(i)[1]
+        return [remote(held.at[i, t], dst.at[t], relay_out.at[i], recv.at[i], (origin + 1, core)) for t in range(2)]
 
     def start_ahead(i):
         @pl.when(jnp.logical_not(relays))
@@ -154,7 +156,8 @@
 
         @pl.when(relays)
         def _():
-            to_relay(i).start()
+            for copy in to_relay(i):
+                copy.start()
 
     def across(h, src, dst, send_sem, recv_sem):
         return remote(rows(h, PAD + src * TOK), rows(h, PAD + dst * TOK), send_sem.at[h], recv_sem.at[h], (c, 1 - core))
@@ -189,12 +192,13 @@
     fill_bias(docs[...], me, bias)
     q_copy.wait()
 
-    def step(i, carry):
-        @pl.when(relays & (i < COPIES))
-        def _():
-            from_relay_in(i)
-            from_relay(i).start()
-
+    def columns(h, g):
+        return pl.ds(pl.multiple_of(h * WIDE + g * HEAD_DIM, HEAD_DIM), HEAD_DIM)
+
+    def joined_queries(h, g):
+        return jnp.concatenate([qbuf[:, columns(h, g + t)] for t in range(JOINED)], axis=0)
+
+    def receive(i):
         @pl.when((c >= 1) & (i < KV_HEADS))
         def _():
             ahead(i).wait_recv()
@@ -211,22 +215,27 @@
             def _():
                 near_across(i).start()
 
-        @pl.when((c >= 2) & (i >= KV_HEADS) & (i < COPIES))
+        @pl.when((c >= 2) & (i >= KV_HEADS) & (core == 1))
         def _():
             ahead(i).wait_recv()
-
-            @pl.when(core == 1)
-            def _():
-                far_across(i - KV_HEADS).start()
-
-        @pl.when((i >= 1) & (i <= KV_HEADS))
-        def _():
-            h = i - 1
-
+            far_across(i - KV_HEADS).start()
+
+        @pl.when(relays)
+        def _():
+            for arrived, copy in zip(into_relay(i), from_relay(i)):
+                arrived.wait_recv()
+                copy.start()
+
+    def into_relay(i):
+        return [remote(held.at[i, t], held.at[i, t], relay_out.at[i], relay_in.at[i, t], (origin + 1, core)) for t in range(2)]
+
+    def near_half(heads):
+        for h in heads:
             @pl.when(c >= 1 - core)
-            def _():
+            def _(h=h):
                 own_across(h).wait_recv()
 
+        for h in heads:
             k, v = kv[h, 0, HALF:], with_ones(kv[h, 1, HALF:])
             for g in range(0, GROUP, JOINED):
                 scores = masked_scores(joined_queries(h, g), k, bias[:, HALF:])
@@ -235,14 +244,17 @@
                 tops[h, at, :] = top
                 sums[h, at, :] = weighted(scores, top, v)
 
-        @pl.when(i > KV_HEADS)
-        def _():
-            h = i - 1 - KV_HEADS
+    def far_half(heads):
+        for h in heads:
+            @pl.when((c >= 2) & (core == 0))
+            def _(h=h):
+                ahead(h + KV_HEADS).wait_recv()
 
             @pl.when(c >= 2 - core)
-            def _():
+            def _(h=h):
                 far_across(h).wait_recv()
 
+        for h in heads:
             k, v = kv[h, 0, :HALF], with_ones(kv[h, 1, :HALF])
             for g in range(0, GROUP, JOINED):
                 scores = masked_scores(joined_queries(h, g), k, bias[:, :HALF])
@@ -255,16 +267,20 @@
                 for t in range(JOINED):
                     o_ref[:, columns(h, g + t)] = result[t * TOK:(t + 1) * TOK]
 
+    def step(i, carry):
+        @pl.when(i < COPIES)
+        def _():
+            receive(i)
+
+        @pl.when((i >= 2) & (i <= KV_HEADS) & (i % 2 == 0))
+        def _():
+            near_half((i - 2, i - 1))
+
+        @pl.when(i > KV_HEADS)
+        def _():
+            far_half((i - 1 - KV_HEADS,))
+
         return carry
-
-    def columns(h, g):
-        return pl.ds(pl.multiple_of(h * WIDE + g * HEAD_DIM, HEAD_DIM), HEAD_DIM)
-
-    def joined_queries(h, g):
-        return jnp.concatenate([qbuf[:, columns(h, g + t)] for t in range(JOINED)], axis=0)
-
-    def from_relay_in(i):
-        remote(held.at[i], held.at[i], relay_out.at[i], relay_in.at[i], (origin + 1, core)).wait_recv()
 
     lax.fori_loop(0, COPIES + 1, step, 0)
 
@@ -275,7 +291,8 @@
 
         @pl.when(relays)
         def _():
-            from_relay(i).wait_send()
+            for copy in from_relay(i):
+                copy.wait_send()
 
         @pl.when((i < KV_HEADS) & (c >= core))
         def _():
@@ -310,7 +327,7 @@
             pltpu.SemaphoreType.DMA,
             pltpu.SemaphoreType.DMA,
             pltpu.SemaphoreType.DMA((KV_HEADS, 2)),
-        ] + [pltpu.SemaphoreType.DMA((COPIES,))] * 4 + [per_head] * 4,
+        ] + [pltpu.SemaphoreType.DMA((COPIES,))] * 3 + [pltpu.SemaphoreType.DMA((COPIES, 2))] + [per_head] * 4,
         compiler_params=pltpu.CompilerParams(
             collective_id=0, has_side_effects=True, vmem_limit_bytes=32 * 1024 * 1024),
     )(*[pltpu.with_memory_space_constraint(x, pltpu.HBM) for x in (doc_lengths.reshape(8, 128), queries, keys, values)])

time: 30.7 us -> 30.1 us (0.980)
  Pallas kernels: 29.4 us -> 28.8 us
    pallas_call x1, Pallas kernels: 29.4 us -> 28.8 us  [local(): pl.pallas_call(functools.partial(kernel, n), out_shape=pltpu.VMEM(queries...]
where the time goes in v3:
time: 30.1 us; the launch traced here: 30 us
  Pallas kernels  28.8 us (96%)
  local copies, waits for them, and re-layouts  1.15 us (4%)
    pallas_call x1, Pallas kernels, local(): pl.pallas_call(functools.partial(kernel, n), out_shape=pltpu.VMEM(queries...  28.8 us
    unnamed x1, local copies, waits for them, and re-layouts  1.15 us

profile of v3, /device:TPU:16, one launch (start us, length us, event | category | flops | bytes accessed | tf_op | source)
XLA Modules:
  0.0 30.0 jit_solution(319926642849775556)
XLA Ops:
  0.0 28.8 %shard_map.46 = bf16[96,8192]{1,0:T(8,128)(2,1)S(1)} custom-call(s32[8,128]{1,0:T(8,128)} %bitcast.1, bf16[96,8192]{1,0:T(8,128)(2,1)} %q_hbm.1, bf16[96,1024]{1,0:T(8,128)(2,1)} %k_hbm.1, bf16[96,1024]{1,0:T(8,128)(2,1)} %v_hbm.1), custom_call_target="tpu_custom_call" | custom-call | tf_op jit(solution)/shard_map/pallas_call | solution.py:314
  28.8 1.1 %copy.6 = bf16[96,8192]{1,0:T(8,128)(2,1)} copy(bf16[96,8192]{1,0:T(8,128)(2,1)S(1)} %shard_map.46) | data formatting | bytes 3145728
